TPU v7x, 32 devices: a whole 2x2x4 slice. The times are simulated.
32 devices in a mesh: rep: 2 (over y), dev: 4 (over z), col: 4 (over x, core).
Axes of the slice: x: 2, y: 2, z: 4, core: 2. Of those that a mesh axis runs over, the one named last changes fastest.
Arguments:
- queries: bfloat16 [256, 8192], P(('rep', 'dev'), 'col'), parts along dimension 0
- kv_pages: bfloat16 [768, 8, 2, 128, 128], P(('rep', 'dev'), 'col'), parts along dimension 0
- page_table: int32 [256, 3], P(('rep', 'dev')), parts along dimension 0, may hold values from 0 to 95, as said below
- seq_lengths: int32 [256], P(('rep', 'dev')), parts along dimension 0, may hold values from 2 to 384, as said below
- ffn_seat: int32 [256], P('rep'), parts along dimension 0, may hold values from 0 to 127, each once
- resid: bfloat16 [256, 8192], P(('rep', 'col'), 'dev'), parts along dimension 0, may hold values from -6 to 6
- w_out: bfloat16 [8192, 8192], P('col', 'dev'), may hold values from -0.0625 to 0.0625
- norm_gain: float32 [8192], P('dev'), may hold values from 0.25 to 1.75
- w_gate: bfloat16 [8192, 14336], P('dev', 'col'), may hold values from -0.0625 to 0.0625
- w_up: bfloat16 [8192, 14336], P('dev', 'col'), may hold values from -0.0625 to 0.0625
- w_down: bfloat16 [14336, 8192], P('col', 'dev'), may hold values from -0.046875 to 0.046875
Outputs:
- layer_out: bfloat16 [256, 8192], P(('rep', 'col'), 'dev'), parts along dimension 0
There are 2 independent parts, one for each index of `rep`. A program takes and returns all parts, laid end to end along the dimension named above; an argument that names none is the same for every part. Nothing has to cross between parts.
Inputs may be any that keep to these rules, and one draw needn't show every extreme that they name: `page_table`: the 32 rows of one dev index hold each block 0 to 95 of that index's pool exactly once. `seq_lengths`: the first sequence has 384 cached tokens.
All inputs are finite; a program needn't handle non-finite values.
Results may differ from a plain program's by a relative error of at most 0.017.
Values may be sent and summed in bfloat16 or wider, within the bound.
A program may use at most 128 MiB of HBM per device.

v0:
```python
import jax
import jax.numpy as jnp
from jax import lax
from jax.sharding import PartitionSpec as P


def on_device(
    queries,
    kv_pages,
    page_table,
    seq_lengths,
    ffn_seat,
    resid,
    w_out,
    norm_gain,
    w_gate,
    w_up,
    w_down,
):
    seq_count = queries.shape[0]
    kv_local = kv_pages.shape[1]
    head_dim = kv_pages.shape[4]
    group_size = queries.shape[1] // (kv_local * head_dim)
    kv_blocks = kv_pages[page_table]
    key_span = kv_blocks.shape[1] * kv_blocks.shape[4]
    key_rows = (
        kv_blocks[:, :, :, 0]
        .transpose(0, 2, 1, 3, 4)
        .reshape(seq_count, kv_local, key_span, head_dim)
    )
    value_rows = (
        kv_blocks[:, :, :, 1]
        .transpose(0, 2, 1, 3, 4)
        .reshape(seq_count, kv_local, key_span, head_dim)
    )
    query_heads = queries.reshape(seq_count, kv_local, group_size, head_dim)
    scores = jnp.einsum(
        "skgd,sktd->skgt", query_heads, key_rows, preferred_element_type=jnp.float32
    ) * head_dim ** (-0.5)
    live_mask = jnp.arange(key_span)[None, :] < seq_lengths[:, None]
    scores = jnp.where(live_mask[:, None, None, :], scores, -1e30)
    top = jnp.max(scores, axis=-1, keepdims=True)
    expo = jnp.exp(scores - top)
    weights = (expo / jnp.sum(expo, axis=-1, keepdims=True)).astype(jnp.bfloat16)
    attended = jnp.einsum(
        "skgt,sktd->skgd", weights, value_rows, preferred_element_type=jnp.float32
    )
    attended = attended.astype(jnp.bfloat16).reshape(seq_count, -1)
    projected = jnp.dot(
        lax.all_gather(attended, "dev", axis=0, tiled=True),
        w_out,
        preferred_element_type=jnp.float32,
    )
    placed = jnp.zeros_like(projected).at[ffn_seat].set(projected)
    update = lax.psum_scatter(
        placed.astype(jnp.bfloat16), "col", scatter_dimension=0, tiled=True
    ).astype(jnp.float32)
    stream = resid.astype(jnp.float32) + update
    sq_total = lax.psum(jnp.sum(stream * stream, axis=1), "dev")
    full_width = stream.shape[1] * lax.axis_size("dev")
    normed = (
        stream * lax.rsqrt(sq_total / full_width + 1e-05)[:, None] * norm_gain[None, :]
    ).astype(jnp.bfloat16)
    block_rows = lax.all_gather(normed, "col", axis=0, tiled=True)
    gate_part = jnp.dot(block_rows, w_gate, preferred_element_type=jnp.float32)
    up_part = jnp.dot(block_rows, w_up, preferred_element_type=jnp.float32)
    gate_up = jnp.concatenate([gate_part, up_part], axis=1)
    half_width = w_gate.shape[1]
    shared_sums = lax.psum_scatter(
        gate_up.astype(jnp.bfloat16), "dev", scatter_dimension=0, tiled=True
    ).astype(jnp.float32)
    hidden_share = (jax.nn.silu(shared_sums[:, :half_width]) * shared_sums[:, half_width:]).astype(
        jnp.bfloat16
    )
    hidden = lax.all_gather(hidden_share, "dev", axis=0, tiled=True)
    ffn_out = lax.psum_scatter(
        jnp.dot(hidden, w_down, preferred_element_type=jnp.float32).astype(jnp.bfloat16),
        "col",
        scatter_dimension=0,
        tiled=True,
    ).astype(jnp.float32)
    return (stream + ffn_out).astype(jnp.bfloat16)


def solution(mesh):
    in_specs = (
        P(("rep", "dev"), "col"),
        P(("rep", "dev"), "col", None, None, None),
        P(("rep", "dev"), None),
        P(("rep", "dev")),
        P("rep"),
        P(("rep", "col"), "dev"),
        P("col", "dev"),
        P("dev"),
        P("dev", "col"),
        P("dev", "col"),
        P("col", "dev"),
    )
    out_specs = P(("rep", "col"), "dev")
    return jax.shard_map(
        on_device, mesh=mesh, in_specs=in_specs, out_specs=out_specs, check_vma=False
    )
```

profile of v0, /device:TPU:0, one launch (start us, length us, event | category | flops | bytes accessed | tf_op | source)
XLA Modules:
  0.0 218.6 jit_solution(14444316653443344116)
XLA Ops:
  7.4 11.5 %gather_fusion = bf16[96,2,2,128,128]{4,3,2,1,0:T(8,128)(2,1)} fusion(bf16[96,2,2,128,128]{4,3,2,1,0:T(8,128)(2,1)} %param.12, s32[1024]{0:T(1024)S(1)} %pad_clamp_fusion), kind=kCustom, calls=%fused_computation | custom fusion | bytes 25166208 | tf_op jit(solution)/shard_map/gather | solution.py:24
  18.9 5.3 %fusion.9 = (bf16[32,3,2,1,128,128]{5,4,3,2,1,0:T(8,128)(2,1)S(1)}, bf16[32,3,2,1,128,128]{5,4,3,2,1,0:T(8,128)(2,1)S(1)}) fusion(bf16[32,3,2,2,128,128]{5,4,3,2,1,0:T(8,128)(2,1)} %bitcast.34), kind=kLoop, calls=%fused_computation.29 | loop fusion | bytes 25165824 | tf_op jit(solution)/shard_map/slice | solution.py:27
  24.3 2.6 %copy.18 = bf16[32,3,2,1,128,128]{5,4,1,2,0,3:T(8,128)(2,1)S(1)} copy(bf16[32,3,2,1,128,128]{5,4,3,2,1,0:T(8,128)(2,1)S(1)} %get-tuple-element.5) | data formatting | bytes 12582912
  27.0 2.3 %fusion.4 = f32[32,2,8,384]{3,2,1,0:T(8,128)S(1)} fusion(bf16[32,2,384,128]{3,2,1,0:T(8,128)(2,1)S(1)} %bitcast.35, bf16[32,2,8,128]{3,2,1,0:T(8,128)(2,1)S(1)} %bitcast.37, pred[32,384]{1,0:T(8,128)(4,1)S(1)} %iota_compare_fusion), kind=kOutput, calls=%fused_computation.11 | convolution fusion | flops 50724864 | bytes 7221248 | tf_op jit(solution)/shard_map/skgd,sktd->skgt/dot_general | solution.py:37
  29.6 4.0 %copy.19 = bf16[32,3,2,1,128,128]{5,4,1,2,0,3:T(8,128)(2,1)} copy(bf16[32,3,2,1,128,128]{5,4,3,2,1,0:T(8,128)(2,1)S(1)} %get-tuple-element.6) | data formatting | bytes 12582912
  33.7 4.5 %convolution_convert_fusion.3 = bf16[32,2,8,128]{3,2,1,0:T(8,128)(2,1)S(1)} fusion(bf16[32,2,384,128]{3,2,1,0:T(8,128)(2,1)} %bitcast.36, f32[32,2,8]{2,1,0:T(2,128)S(1)} %fusion.10, f32[32,2,8,384]{3,2,1,0:T(8,128)} %copy-done), kind=kOutput, calls=%fused_computation.12 | convolution fusion | flops 50987904 | bytes 7211008 | tf_op jit(solution)/shard_map/skgt,sktd->skgd/dot_general | solution.py:45
  38.2 17.4 %all_gather.9 = bf16[128,2048]{1,0:T(8,128)(2,1)S(1)} all-gather(bf16[32,2048]{1,0:T(8,128)(2,1)S(1)} %bitcast.38), channel_id=1, replica_groups=mesh['rep'=2,'dev'=4,'col'=4] {'dev'}, dimensions={0}, use_global_device_ids=true | all-gather | bytes 655360 | tf_op jit(solution)/shard_map/all_gather | solution.py:50
  55.6 4.7 %fusion.11 = f32[128,2048]{1,0:T(8,128)S(1)} fusion(bf16[128,2048]{1,0:T(8,128)(2,1)S(1)} %all_gather.9, bf16[2048,2048]{1,0:T(8,128)(2,1)} %param.17), kind=kOutput, calls=%fused_computation.31 | convolution fusion | flops 1073741824 | bytes 9961472 | tf_op jit(solution)/shard_map/dot_general | solution.py:49
  60.3 1.5 scatter_custom_fusion
  61.8 0.9 convert_element_type.37
  62.8 23.5 %reduce-scatter.4.cloned.1.call-done = bf16[32,2048]{1,0:T(8,128)(2,1)} async-done(((bf16[128,2048]{1,0:T(8,128)(2,1)}), bf16[32,2048]{1,0:T(8,128)(2,1)}) %reduce-scatter.4.cloned.1.call-update) | async-done | bytes 131088 | tf_op jit(solution)/shard_map/reduce_scatter | solution.py:55
  86.3 1.1 multiply_reduce_fusion
  87.3 11.7 %psum.7 = f32[32]{0:T(128)S(1)} all-reduce(f32[32]{0:T(128)S(1)} %multiply_reduce_fusion), channel_id=1, replica_groups=mesh['rep'=2,'dev'=4,'col'=4] {'dev'}, use_global_device_ids=true, to_apply=%region_5.6 | all-reduce | flops 32 | bytes 256 | tf_op jit(solution)/shard_map/psum | solution.py:59
  99.0 1.0 multiply_convert_fusion
  100.0 6.7 %all_gather.10 = bf16[128,2048]{1,0:T(8,128)(2,1)S(1)} all-gather(bf16[32,2048]{1,0:T(8,128)(2,1)S(1)} %multiply_convert_fusion), channel_id=1, replica_groups=mesh['rep'=2,'dev'=4,'col'=4] {'col'}, dimensions={0}, use_global_device_ids=true | all-gather | bytes 655360 | tf_op jit(solution)/shard_map/all_gather | solution.py:64
  106.7 7.3 %convolution_convert_fusion = bf16[128,3584]{1,0:T(8,128)(2,1)S(1)} fusion(bf16[128,2048]{1,0:T(8,128)(2,1)S(1)} %all_gather.10, bf16[2048,3584]{1,0:T(8,128)(2,1)} %param.20), kind=kOutput, calls=%fused_computation.3 | convolution fusion | flops 1879506944 | bytes 16121856 | tf_op jit(solution)/shard_map/dot_general | solution.py:66
  114.0 7.3 %convolution_convert_fusion.1 = bf16[128,3584]{1,0:T(8,128)(2,1)S(1)} fusion(bf16[128,2048]{1,0:T(8,128)(2,1)S(1)} %all_gather.10, bf16[2048,3584]{1,0:T(8,128)(2,1)} %param.19), kind=kOutput, calls=%fused_computation.4 | convolution fusion | flops 1879506944 | bytes 16121856 | tf_op jit(solution)/shard_map/dot_general | solution.py:65
  121.3 1.4 pad_maximum_fusion
  122.8 37.5 %reduce-scatter.6.cloned.1.call-done = bf16[32,7168]{1,0:T(8,128)(2,1)} async-done(((bf16[128,7168]{1,0:T(8,128)(2,1)}), bf16[32,7168]{1,0:T(8,128)(2,1)}) %reduce-scatter.6.cloned.1.call-update) | async-done | bytes 458768 | tf_op jit(solution)/shard_map/reduce_scatter | solution.py:69
  160.3 1.1 convert_element_type.40
  161.5 19.1 %all_gather.11 = bf16[128,3584]{1,0:T(8,128)(2,1)S(1)} all-gather(bf16[32,3584]{1,0:T(8,128)(2,1)S(1)} %fusion.7), channel_id=1, replica_groups=mesh['rep'=2,'dev'=4,'col'=4] {'dev'}, dimensions={0}, use_global_device_ids=true | all-gather | bytes 1146880 | tf_op jit(solution)/shard_map/all_gather | solution.py:75
  180.6 8.3 %convolution_convert_fusion.2 = bf16[128,2048]{1,0:T(8,128)(2,1)} fusion(bf16[128,3584]{1,0:T(8,128)(2,1)S(1)} %all_gather.11, bf16[3584,2048]{1,0:T(8,128)(2,1)} %param.21), kind=kOutput, calls=%fused_computation.5 | convolution fusion | flops 1879310336 | bytes 16121856 | tf_op jit(solution)/shard_map/dot_general | solution.py:77
  189.0 21.5 %reduce-scatter.8.cloned.1.call-done = bf16[32,2048]{1,0:T(8,128)(2,1)} async-done(((bf16[128,2048]{1,0:T(8,128)(2,1)}), bf16[32,2048]{1,0:T(8,128)(2,1)}) %reduce-scatter.8.cloned.1.call-update) | async-done | bytes 131088 | tf_op jit(solution)/shard_map/reduce_scatter | solution.py:76
  210.4 1.6 add_convert_fusion
  (31 shorter events, 1.7 us)
Async XLA Ops:
  6.5 79.7 %reduce-scatter.4.cloned.1.call-start = ((), (), s32[]{:S(2)}) async-start(), calls=%async_computation.3 | async-start | bytes 655360 | tf_op jit(solution)/shard_map/reduce_scatter | solution.py:55
  24.2 2.7 %copy-start.3 = (bf16[32,2048]{1,0:T(8,128)(2,1)S(1)}, bf16[32,2048]{1,0:T(8,128)(2,1)}, u32[]{:S(2)}) copy-start(bf16[32,2048]{1,0:T(8,128)(2,1)} %param.11) | copy-start | bytes 393220
  24.2 2.7 %copy-start.5 = (s32[32]{0:T(128)S(1)}, s32[32]{0:T(128)}, u32[]{:S(2)}) copy-start(s32[32]{0:T(128)} %param.14) | copy-start | bytes 388
  29.3 4.4 %copy-start = (f32[32,2,8,384]{3,2,1,0:T(8,128)}, f32[32,2,8,384]{3,2,1,0:T(8,128)S(1)}, u32[]{:S(2)}) copy-start(f32[32,2,8,384]{3,2,1,0:T(8,128)S(1)} %fusion.4) | copy-start | bytes 2359300
  29.6 26.0 %copy-start.6 = (s32[128]{0:T(128)S(1)}, s32[128]{0:T(128)}, u32[]{:S(2)}) copy-start(s32[128]{0:T(128)} %param.15) | copy-start | bytes 1540
  55.6 30.7 %copy-start.1 = (bf16[32,2048]{1,0:T(8,128)(2,1)S(1)}, bf16[32,2048]{1,0:T(8,128)(2,1)}, u32[]{:S(2)}) copy-start(bf16[32,2048]{1,0:T(8,128)(2,1)} %param.16) | copy-start | bytes 393220
  55.6 43.4 %copy-start.4 = (f32[2048]{0:T(1024)S(1)}, f32[2048]{0:T(1024)}, u32[]{:S(2)}) copy-start(f32[2048]{0:T(1024)} %param.18) | copy-start | bytes 24580
  62.7 97.6 %reduce-scatter.6.cloned.1.call-start = ((), (), s32[]{:S(2)}) async-start(), calls=%async_computation.4 | async-start | bytes 2293760 | tf_op jit(solution)/shard_map/reduce_scatter | solution.py:69
  122.7 87.7 %reduce-scatter.8.cloned.1.call-start = ((), (), s32[]{:S(2)}) async-start(), calls=%async_computation.5 | async-start | bytes 655360 | tf_op jit(solution)/shard_map/reduce_scatter | solution.py:76
  180.6 29.9 %copy-start.2 = (bf16[32,2048]{1,0:T(8,128)(2,1)S(1)}, bf16[32,2048]{1,0:T(8,128)(2,1)}, u32[]{:S(2)}) copy-start(bf16[32,2048]{1,0:T(8,128)(2,1)} %reduce-scatter.4.cloned.1.call-done) | copy-start | bytes 393220
Sparse Core Ops, SparseCore 0:
  62.8 23.4 reduce-scatter.3
  122.8 37.3 reduce-scatter.5
  189.1 21.3 reduce-scatter.7
where the time goes:
time: 219 us
  waiting for transfers between devices  82.6 us (38%)
  blocking collectives  54.8 us (25%)
  matrix products  34.4 us (16%)
  local copies, waits for them, and re-layouts  25.2 us (12%)
  between operations  13.3 us (6%)
  other arithmetic  8.25 us (4%)
    reduce_scatter x1, waiting for transfers between devices, on_device(): lax.psum_scatter(gate_up.astype(jnp.bfloat16), 'dev', scatter_dimension=0...  37.5 us
    reduce_scatter x1, waiting for transfers between devices, on_device(): lax.psum_scatter(placed.astype(jnp.bfloat16), 'col', scatter_dimension=0,...  23.5 us
    reduce_scatter x1, waiting for transfers between devices, on_device(): lax.psum_scatter(jnp.dot(hidden, w_down, preferred_element_type=jnp.float...  21.5 us
    all_gather x1, blocking collectives, on_device(): hidden = lax.all_gather(hidden_share, 'dev', axis=0, tiled=True)  19.1 us
    all_gather x1, blocking collectives, on_device(): lax.all_gather(attended, 'dev', axis=0, tiled=True)  17.4 us
    psum x1, blocking collectives, on_device(): sq_total = lax.psum(jnp.sum(stream * stream, axis=1), 'dev')  11.7 us
    gather x1, local copies, waits for them, and re-layouts, on_device(): kv_blocks = kv_pages[page_table]  11.5 us
    dot_general x1, matrix products, on_device(): jnp.dot(hidden, w_down, preferred_element_type=jnp.float32)  8.35 us
  transfers between devices with their start and end apart: 3, of which 3 were waited for; matrix products, arithmetic and copies ran while one was open for 0% of the time, Pallas kernels for 0%

commit v1 on v0

--- a/solution.py
+++ b/solution.py
@@ -56,7 +56,7 @@
         placed.astype(jnp.bfloat16), "col", scatter_dimension=0, tiled=True
     ).astype(jnp.float32)
     stream = resid.astype(jnp.float32) + update
-    sq_total = lax.psum(jnp.sum(stream * stream, axis=1), "dev")
+    sq_total = jnp.sum(lax.all_gather(jnp.sum(stream * stream, axis=1), "dev"), axis=0)
     full_width = stream.shape[1] * lax.axis_size("dev")
     normed = (
         stream * lax.rsqrt(sq_total / full_width + 1e-05)[:, None] * norm_gain[None, :]

time: 219 us -> 219 us (level)
    psum x1 -> x0, blocking collectives: 11.7 us -> none  [on_device(): sq_total = lax.psum(jnp.sum(stream * stream, axis=1), 'dev')]
    unnamed x0 -> x1, blocking collectives: none -> 11.7 us
    unnamed x18 -> x23, local copies, waits for them, and re-layouts: 6.78 us -> 7.61 us
where the time goes in v1:
time: 219 us
  waiting for transfers between devices  81.3 us (37%)
  blocking collectives  54.8 us (25%)
  matrix products  34.4 us (16%)
  local copies, waits for them, and re-layouts  26.2 us (12%)
  between operations  13.9 us (6%)
  other arithmetic  8.27 us (4%)
    reduce_scatter x1, waiting for transfers between devices, on_device(): lax.psum_scatter(gate_up.astype(jnp.bfloat16), 'dev', scatter_dimension=0...  37.5 us
    reduce_scatter x1, waiting for transfers between devices, on_device(): lax.psum_scatter(placed.astype(jnp.bfloat16), 'col', scatter_dimension=0,...  22.2 us
    reduce_scatter x1, waiting for transfers between devices, on_device(): lax.psum_scatter(jnp.dot(hidden, w_down, preferred_element_type=jnp.float...  21.5 us
    all_gather x1, blocking collectives, on_device(): hidden = lax.all_gather(hidden_share, 'dev', axis=0, tiled=True)  19.1 us
    all_gather x1, blocking collectives, on_device(): lax.all_gather(attended, 'dev', axis=0, tiled=True)  17.4 us
    unnamed x1, blocking collectives  11.7 us
    gather x1, local copies, waits for them, and re-layouts, on_device(): kv_blocks = kv_pages[page_table]  11.5 us
    dot_general x1, matrix products, on_device(): jnp.dot(hidden, w_down, preferred_element_type=jnp.float32)  8.35 us
  transfers between devices with their start and end apart: 3, of which 3 were waited for; matrix products, arithmetic and copies ran while one was open for 0% of the time, Pallas kernels for 0%

profile of v1, /device:TPU:0, one launch (start us, length us, event | category | flops | bytes accessed | tf_op | source)
XLA Modules:
  0.0 218.9 jit_solution(10186314834505629324)
XLA Ops:
  7.4 11.5 %gather_fusion = bf16[96,2,2,128,128]{4,3,2,1,0:T(8,128)(2,1)} fusion(bf16[96,2,2,128,128]{4,3,2,1,0:T(8,128)(2,1)} %param.12, s32[1024]{0:T(1024)S(1)} %pad_clamp_fusion), kind=kCustom, calls=%fused_computation | custom fusion | bytes 25166208 | tf_op jit(solution)/shard_map/gather | solution.py:24
  18.9 5.3 %fusion.9 = (bf16[32,3,2,1,128,128]{5,4,3,2,1,0:T(8,128)(2,1)S(1)}, bf16[32,3,2,1,128,128]{5,4,3,2,1,0:T(8,128)(2,1)S(1)}) fusion(bf16[32,3,2,2,128,128]{5,4,3,2,1,0:T(8,128)(2,1)} %bitcast.35), kind=kLoop, calls=%fused_computation.29 | loop fusion | bytes 25165824 | tf_op jit(solution)/shard_map/slice | solution.py:27
  24.3 2.6 %copy.18 = bf16[32,3,2,1,128,128]{5,4,1,2,0,3:T(8,128)(2,1)S(1)} copy(bf16[32,3,2,1,128,128]{5,4,3,2,1,0:T(8,128)(2,1)S(1)} %get-tuple-element.5) | data formatting | bytes 12582912
  27.0 2.3 %fusion.4 = f32[32,2,8,384]{3,2,1,0:T(8,128)S(1)} fusion(bf16[32,2,384,128]{3,2,1,0:T(8,128)(2,1)S(1)} %bitcast.36, bf16[32,2,8,128]{3,2,1,0:T(8,128)(2,1)S(1)} %bitcast.38, pred[32,384]{1,0:T(8,128)(4,1)S(1)} %iota_compare_fusion), kind=kOutput, calls=%fused_computation.11 | convolution fusion | flops 50724864 | bytes 7221248 | tf_op jit(solution)/shard_map/skgd,sktd->skgt/dot_general | solution.py:37
  29.6 4.0 %copy.19 = bf16[32,3,2,1,128,128]{5,4,1,2,0,3:T(8,128)(2,1)} copy(bf16[32,3,2,1,128,128]{5,4,3,2,1,0:T(8,128)(2,1)S(1)} %get-tuple-element.6) | data formatting | bytes 12582912
  33.7 4.5 %convolution_convert_fusion.3 = bf16[32,2,8,128]{3,2,1,0:T(8,128)(2,1)S(1)} fusion(bf16[32,2,384,128]{3,2,1,0:T(8,128)(2,1)} %bitcast.37, f32[32,2,8]{2,1,0:T(2,128)S(1)} %fusion.10, f32[32,2,8,384]{3,2,1,0:T(8,128)} %copy-done), kind=kOutput, calls=%fused_computation.12 | convolution fusion | flops 50987904 | bytes 7211008 | tf_op jit(solution)/shard_map/skgt,sktd->skgd/dot_general | solution.py:45
  38.2 17.4 %all_gather.15 = bf16[128,2048]{1,0:T(8,128)(2,1)S(1)} all-gather(bf16[32,2048]{1,0:T(8,128)(2,1)S(1)} %bitcast.39), channel_id=1, replica_groups=mesh['rep'=2,'dev'=4,'col'=4] {'dev'}, dimensions={0}, use_global_device_ids=true | all-gather | bytes 655360 | tf_op jit(solution)/shard_map/all_gather | solution.py:50
  55.6 4.7 %fusion.11 = f32[128,2048]{1,0:T(8,128)S(1)} fusion(bf16[128,2048]{1,0:T(8,128)(2,1)S(1)} %all_gather.15, bf16[2048,2048]{1,0:T(8,128)(2,1)} %param.17), kind=kOutput, calls=%fused_computation.31 | convolution fusion | flops 1073741824 | bytes 9961472 | tf_op jit(solution)/shard_map/dot_general | solution.py:49
  60.4 1.5 scatter_custom_fusion
  61.8 0.9 convert_element_type.37
  64.0 22.2 %reduce-scatter.4.cloned.1.call-done = bf16[32,2048]{1,0:T(8,128)(2,1)} async-done(((bf16[128,2048]{1,0:T(8,128)(2,1)}), bf16[32,2048]{1,0:T(8,128)(2,1)}) %reduce-scatter.4.cloned.1.call-update) | async-done | bytes 131088 | tf_op jit(solution)/shard_map/reduce_scatter | solution.py:55
  86.3 1.1 multiply_reduce_fusion
  87.6 11.7 %all-reduce = f32[128]{0:T(128)S(1)} all-reduce(f32[128]{0:T(128)S(1)} %dynamic-update-slice), channel_id=2, replica_groups=mesh['rep'=2,'dev'=4,'col'=4] {'dev'}, use_global_device_ids=true, to_apply=%add | all-reduce | flops 128 | bytes 1024
  99.4 1.0 multiply_convert_fusion
  100.4 6.7 %all_gather.18 = bf16[128,2048]{1,0:T(8,128)(2,1)S(1)} all-gather(bf16[32,2048]{1,0:T(8,128)(2,1)S(1)} %multiply_convert_fusion), channel_id=1, replica_groups=mesh['rep'=2,'dev'=4,'col'=4] {'col'}, dimensions={0}, use_global_device_ids=true | all-gather | bytes 655360 | tf_op jit(solution)/shard_map/all_gather | solution.py:64
  107.1 7.3 %convolution_convert_fusion = bf16[128,3584]{1,0:T(8,128)(2,1)S(1)} fusion(bf16[128,2048]{1,0:T(8,128)(2,1)S(1)} %all_gather.18, bf16[2048,3584]{1,0:T(8,128)(2,1)} %param.20), kind=kOutput, calls=%fused_computation.3 | convolution fusion | flops 1879506944 | bytes 16121856 | tf_op jit(solution)/shard_map/dot_general | solution.py:66
  114.3 7.3 %convolution_convert_fusion.1 = bf16[128,3584]{1,0:T(8,128)(2,1)S(1)} fusion(bf16[128,2048]{1,0:T(8,128)(2,1)S(1)} %all_gather.18, bf16[2048,3584]{1,0:T(8,128)(2,1)} %param.19), kind=kOutput, calls=%fused_computation.4 | convolution fusion | flops 1879506944 | bytes 16121856 | tf_op jit(solution)/shard_map/dot_general | solution.py:65
  121.6 1.4 pad_maximum_fusion
  123.1 37.5 %reduce-scatter.6.cloned.1.call-done = bf16[32,7168]{1,0:T(8,128)(2,1)} async-done(((bf16[128,7168]{1,0:T(8,128)(2,1)}), bf16[32,7168]{1,0:T(8,128)(2,1)}) %reduce-scatter.6.cloned.1.call-update) | async-done | bytes 458768 | tf_op jit(solution)/shard_map/reduce_scatter | solution.py:69
  160.6 1.1 convert_element_type.40
  161.8 19.1 %all_gather.19 = bf16[128,3584]{1,0:T(8,128)(2,1)S(1)} all-gather(bf16[32,3584]{1,0:T(8,128)(2,1)S(1)} %fusion.7), channel_id=1, replica_groups=mesh['rep'=2,'dev'=4,'col'=4] {'dev'}, dimensions={0}, use_global_device_ids=true | all-gather | bytes 1146880 | tf_op jit(solution)/shard_map/all_gather | solution.py:75
  181.0 8.3 %convolution_convert_fusion.2 = bf16[128,2048]{1,0:T(8,128)(2,1)} fusion(bf16[128,3584]{1,0:T(8,128)(2,1)S(1)} %all_gather.19, bf16[3584,2048]{1,0:T(8,128)(2,1)} %param.21), kind=kOutput, calls=%fused_computation.5 | convolution fusion | flops 1879310336 | bytes 16121856 | tf_op jit(solution)/shard_map/dot_general | solution.py:77
  189.3 21.5 %reduce-scatter.8.cloned.1.call-done = bf16[32,2048]{1,0:T(8,128)(2,1)} async-done(((bf16[128,2048]{1,0:T(8,128)(2,1)}), bf16[32,2048]{1,0:T(8,128)(2,1)}) %reduce-scatter.8.cloned.1.call-update) | async-done | bytes 131088 | tf_op jit(solution)/shard_map/reduce_scatter | solution.py:76
  210.8 1.6 add_convert_fusion
  (38 shorter events, 2.6 us)
Async XLA Ops:
  6.5 79.7 %reduce-scatter.4.cloned.1.call-start = ((), (), s32[]{:S(2)}) async-start(), calls=%async_computation.3 | async-start | bytes 655360 | tf_op jit(solution)/shard_map/reduce_scatter | solution.py:55
  24.2 2.7 %copy-start.3 = (bf16[32,2048]{1,0:T(8,128)(2,1)S(1)}, bf16[32,2048]{1,0:T(8,128)(2,1)}, u32[]{:S(2)}) copy-start(bf16[32,2048]{1,0:T(8,128)(2,1)} %param.11) | copy-start | bytes 393220
  24.2 2.7 %copy-start.5 = (s32[32]{0:T(128)S(1)}, s32[32]{0:T(128)}, u32[]{:S(2)}) copy-start(s32[32]{0:T(128)} %param.14) | copy-start | bytes 388
  29.3 4.4 %copy-start = (f32[32,2,8,384]{3,2,1,0:T(8,128)}, f32[32,2,8,384]{3,2,1,0:T(8,128)S(1)}, u32[]{:S(2)}) copy-start(f32[32,2,8,384]{3,2,1,0:T(8,128)S(1)} %fusion.4) | copy-start | bytes 2359300
  29.6 26.0 %copy-start.6 = (s32[128]{0:T(128)S(1)}, s32[128]{0:T(128)}, u32[]{:S(2)}) copy-start(s32[128]{0:T(128)} %param.15) | copy-start | bytes 1540
  55.6 7.2 %copy-start.7 = (u32[32]{0:T(128)S(1)}, u32[32]{0:T(128)}, u32[]{:S(2)}) copy-start(u32[32]{0:T(128)} %constant.27) | copy-start | bytes 388
  55.6 30.6 %copy-start.1 = (bf16[32,2048]{1,0:T(8,128)(2,1)S(1)}, bf16[32,2048]{1,0:T(8,128)(2,1)}, u32[]{:S(2)}) copy-start(bf16[32,2048]{1,0:T(8,128)(2,1)} %param.16) | copy-start | bytes 393220
  55.6 43.7 %copy-start.4 = (f32[2048]{0:T(1024)S(1)}, f32[2048]{0:T(1024)}, u32[]{:S(2)}) copy-start(f32[2048]{0:T(1024)} %param.18) | copy-start | bytes 24580
  62.7 97.9 %reduce-scatter.6.cloned.1.call-start = ((), (), s32[]{:S(2)}) async-start(), calls=%async_computation.4 | async-start | bytes 2293760 | tf_op jit(solution)/shard_map/reduce_scatter | solution.py:69
  123.1 87.7 %reduce-scatter.8.cloned.1.call-start = ((), (), s32[]{:S(2)}) async-start(), calls=%async_computation.5 | async-start | bytes 655360 | tf_op jit(solution)/shard_map/reduce_scatter | solution.py:76
  180.9 29.9 %copy-start.2 = (bf16[32,2048]{1,0:T(8,128)(2,1)S(1)}, bf16[32,2048]{1,0:T(8,128)(2,1)}, u32[]{:S(2)}) copy-start(bf16[32,2048]{1,0:T(8,128)(2,1)} %reduce-scatter.4.cloned.1.call-done) | copy-start | bytes 393220
Sparse Core Ops, SparseCore 0:
  62.8 23.3 reduce-scatter.3
  123.2 37.3 reduce-scatter.5
  189.4 21.3 reduce-scatter.7
